TPU v7x, 32 devices: a whole 2x2x4 slice. The times are simulated.
32 devices in a mesh: grp: 4 (over y, x), mem: 8 (over z, core).
Axes of the slice: x: 2, y: 2, z: 4, core: 2. Of those that a mesh axis runs over, the one named last changes fastest.
Arguments:
- weight: bfloat16 [2, 16384, 16384], P(None, None, ('grp', 'mem')), may hold values from -0.046875 to 0.046875
- activation: bfloat16 [2, 16384, 512], P(None, ('grp', 'mem')), may hold values from -6 to 6
- points: int32 [4], replicated, may hold values from 0 to 3, each once
Outputs:
- share: float32 [4, 16384, 512], P('grp', 'mem')
Inputs may be any that keep to these rules, and one draw needn't show every extreme that they name: A permutation of 0 to 3; group g evaluates at points[g] + 1.
All inputs are finite; a program needn't handle non-finite values.
Results may differ from a plain program's by a relative error of at most 0.0042.
Values may be sent and summed in bfloat16 or wider, within the bound.
A program may use at most 320 MiB of HBM per device.

v0:
```python
import jax
import jax.numpy as jnp
from jax import lax
from jax.sharding import PartitionSpec as P


def code_stack(raw_blocks, factors):
    total = factors[:, 0, None, None] * raw_blocks[0].astype(jnp.float32)[None]
    for block in range(1, raw_blocks.shape[0]):
        total = total + factors[:, block, None, None] * raw_blocks[block].astype(jnp.float32)[None]
    return total.astype(jnp.bfloat16)


def per_device(weight, activation, points):
    groups = lax.axis_size("grp")
    blocks = weight.shape[0]
    splits = activation.shape[0]
    anchors = (points + 1).astype(jnp.float32) / groups
    factors = anchors[:, None] ** jnp.arange(blocks, dtype=jnp.float32)[None, :]
    lifts_all = anchors[:, None] ** (jnp.arange(splits, dtype=jnp.float32) * blocks)[None, :]
    slab = lax.all_to_all(weight, "mem", split_axis=1, concat_axis=2, tiled=True)
    block_input = lax.all_gather(activation, "mem", axis=1, tiled=True)
    coded_weight = code_stack(slab, factors)
    coded_input = code_stack(block_input, lifts_all)
    return lax.psum_scatter(
        jnp.einsum("grk,gkc->grc", coded_weight, coded_input, preferred_element_type=jnp.float32),
        "grp",
        scatter_dimension=0,
        tiled=True,
    )


def solution(mesh):
    placed = (P(None, None, ("grp", "mem")), P(None, ("grp", "mem"), None), P())
    return jax.shard_map(
        per_device, mesh=mesh, in_specs=placed, out_specs=P("grp", "mem", None), check_vma=False
    )
```

profile of v0, /device:TPU:0, one launch (start us, length us, event | category | flops | bytes accessed | tf_op | source)
XLA Modules:
  0.0 1254.2 jit_solution(2382327408538441488)
XLA Ops:
  6.5 60.1 %copy.10 = bf16[2,16384,512]{2,0,1:T(2,128)(2,1)} copy(bf16[2,16384,512]{2,1,0:T(8,128)(2,1)} %param.3) | data formatting | bytes 67108864 | tf_op args[0]
  66.6 0.0 copy-start
  66.6 7.2 all-to-all-start
  73.9 0.0 all-gather.2.cloned.1.call-start
  73.9 0.7 all-gather.2.cloned.1.call-update
  74.6 0.0 reduce-scatter.4.cloned.1.call-start
  74.7 0.0 copy-done
  74.7 0.1 broadcast_power_fusion
  74.8 154.4 %all-gather.2.cloned.1.call-done = bf16[2,4096,512]{2,1,0:T(8,128)(2,1)} async-done(((bf16[2,512,512]{2,1,0:T(8,128)(2,1)}), bf16[2,4096,512]{2,1,0:T(8,128)(2,1)}) %all-gather.2.cloned.1.call-update) | async-done | bytes 8388624 | tf_op jit(solution)/shard_map/all_gather | solution.py:22
  229.1 11.7 fusion.10
  240.9 15.1 %add_convert_fusion.10 = bf16[4,4096,512]{2,1,0:T(8,128)(2,1)} fusion(f32[4096,512]{1,0:T(8,128)} %get-tuple-element.8, f32[4]{0:T(128)S(1)} %get-tuple-element.10, f32[4096,512]{1,0:T(8,128)} %get-tuple-element.7, f32[4]{0:T(128)S(1)} %get-tuple-element.9), kind=kLoop, calls=%fused_computation.6.clone.clone.2 | loop fusion | flops 33554432 | bytes 33554464 | tf_op jit(solution)/shard_map/grk,gkc->grc/dot_general | solution.py:26
  256.0 609.3 %all-to-all-done = bf16[2,16384,512]{2,0,1:T(2,128)(2,1)} async-done(((bf16[2,16384,512]{2,0,1:T(2,128)(2,1)}), bf16[2,16384,512]{2,0,1:T(2,128)(2,1)}, u32[]{:S(2)}, u32[]{:S(2)}) %all-to-all-start) | async-done | bytes 33554464 | tf_op jit(solution)/shard_map/all_to_all | solution.py:21
  865.3 22.7 %copy.11 = bf16[2,16384,512]{2,1,0:T(8,128)(2,1)} copy(bf16[2,16384,512]{2,0,1:T(2,128)(2,1)} %all-to-all-done) | data formatting | bytes 67108864 | tf_op jit(solution)/shard_map/all_to_all | solution.py:21
  888.0 34.1 %slice_convert_fusion.1 = (f32[1,2048,8,512]{3,1,2,0:T(8,128)}, f32[1,2048,8,512]{3,1,2,0:T(8,128)}) fusion(bf16[2,2048,8,512]{3,1,2,0:T(8,128)(2,1)} %bitcast.25), kind=kLoop, calls=%fused_computation.8 | loop fusion | flops 16777216 | bytes 100663296 | tf_op jit(solution)/shard_map/convert_element_type | solution.py:8
  922.1 31.8 %copy.14 = f32[1,2048,8,512]{1,3,2,0:T(8,128)} copy(f32[1,2048,8,512]{3,1,2,0:T(8,128)} %get-tuple-element.6) | data formatting | bytes 67108864 | tf_op jit(solution)/shard_map/convert_element_type | solution.py:10
  953.9 31.1 %copy.15 = f32[2048,4096]{1,0:T(8,128)} copy(f32[2048,4096]{0,1:T(8,128)} %bitcast.26) | data formatting | bytes 67108864 | tf_op jit(solution)/shard_map/convert_element_type | solution.py:10
  985.0 31.8 %copy.12 = f32[1,2048,8,512]{1,3,2,0:T(8,128)} copy(f32[1,2048,8,512]{3,1,2,0:T(8,128)} %get-tuple-element.5) | data formatting | bytes 67108864 | tf_op jit(solution)/shard_map/convert_element_type | solution.py:8
  1016.8 31.1 %copy.13 = f32[2048,4096]{1,0:T(8,128)} copy(f32[2048,4096]{0,1:T(8,128)} %bitcast.27) | data formatting | bytes 67108864 | tf_op jit(solution)/shard_map/convert_element_type | solution.py:8
  1047.9 46.0 %fusion = f32[4,2048,512]{2,1,0:T(8,128)} fusion(f32[2048,4096]{1,0:T(8,128)} %copy.15, f32[4]{0:T(128)S(1)} %get-tuple-element.15, f32[2048,4096]{1,0:T(8,128)} %copy.13, f32[4]{0:T(128)S(1)} %get-tuple-element.16, bf16[4,4096,512]{2,1,0:T(8,128)(2,1)} %add_convert_fusion.10), kind=kOutput, calls=%fused_computation.1 | convolution fusion | flops 34493956096 | bytes 100663328 | tf_op jit(solution)/shard_map/grk,gkc->grc/dot_general | solution.py:26
  1093.9 0.0 reduce-scatter.4.cloned.1.call-update
  1094.0 153.4 %reduce-scatter.4.cloned.1.call-done = f32[1,2048,512]{2,1,0:T(8,128)} async-done(((f32[4,2048,512]{2,1,0:T(8,128)}), f32[1,2048,512]{2,1,0:T(8,128)}) %reduce-scatter.4.cloned.1.call-update) | async-done | bytes 4194320
  (3 shorter events, 0.0 us)
Async XLA Ops:
  66.6 8.0 copy-start
  66.6 798.7 %all-to-all-start = ((bf16[2,16384,512]{2,0,1:T(2,128)(2,1)}), bf16[2,16384,512]{2,0,1:T(2,128)(2,1)}, u32[]{:S(2)}, u32[]{:S(2)}) async-start(bf16[2,16384,512]{2,0,1:T(2,128)(2,1)} %copy.10), calls=%async_computation | async-start | bytes 67108864 | tf_op jit(solution)/shard_map/all_to_all | solution.py:21
  73.9 155.3 %all-gather.2.cloned.1.call-start = ((), (), s32[]{:S(2)}) async-start(), calls=%async_computation.2 | async-start | bytes 9437184 | tf_op jit(solution)/shard_map/all_gather | solution.py:22
  74.6 1172.8 %reduce-scatter.4.cloned.1.call-start = ((), (), s32[]{:S(2)}) async-start(), calls=%async_computation.3 | async-start | bytes 20971520
Sparse Core Ops, SparseCore 0:
  76.3 152.8 all-gather.1
  1094.1 153.2 reduce-scatter.3
where the time goes:
time: 1260 us; the launch traced here: 1250 us
  waiting for transfers between devices  918 us (73%)
  local copies, waits for them, and re-layouts  209 us (17%)
  other arithmetic  60.9 us (5%)
  matrix products  46 us (4%)
  between operations  13.5 us (1%)
    all_to_all x1, waiting for transfers between devices, per_device(): lax.all_to_all(weight, 'mem', split_axis=1, concat_axis=2, tiled=True)  609 us
    all_gather x1, waiting for transfers between devices, per_device(): block_input = lax.all_gather(activation, 'mem', axis=1, tiled=True)  154 us
    unnamed x3, waiting for transfers between devices  154 us
    convert_element_type x2, local copies, waits for them, and re-layouts, code_stack(): raw_blocks[block].astype(jnp.float32)[None]  62.9 us
    convert_element_type x2, local copies, waits for them, and re-layouts, code_stack(): total = factors[:, 0, None, None] * raw_blocks[0].astype(jnp.float32)[None]  62.9 us
    unnamed x3, local copies, waits for them, and re-layouts  60.1 us
    dot_general x1, matrix products, per_device(): jnp.einsum('grk,gkc->grc', coded_weight, coded_input, preferred_element_t...  46 us
    convert_element_type x1, other arithmetic, code_stack(): total = factors[:, 0, None, None] * raw_blocks[0].astype(jnp.float32)[None]  34.1 us
  transfers between devices with their start and end apart: 3, of which 3 were waited for; matrix products, arithmetic and copies ran while one was open for 2% of the time, Pallas kernels for 0%

commit v1 on v0

--- a/solution.py
+++ b/solution.py
@@ -2,6 +2,7 @@
 import jax.numpy as jnp
 from jax import lax
 from jax.sharding import PartitionSpec as P
+from jax.lax import all_to_all, psum
 
 
 def code_stack(raw_blocks, factors):
@@ -19,7 +20,9 @@
     factors = anchors[:, None] ** jnp.arange(blocks, dtype=jnp.float32)[None, :]
     lifts_all = anchors[:, None] ** (jnp.arange(splits, dtype=jnp.float32) * blocks)[None, :]
     slab = lax.all_to_all(weight, "mem", split_axis=1, concat_axis=2, tiled=True)
-    block_input = lax.all_gather(activation, "mem", axis=1, tiled=True)
+    block_input = jnp.concatenate(
+        all_to_all(jnp.stack([activation] * psum(1, "mem"), axis=0), "mem", 0, 0), axis=1
+    )
     coded_weight = code_stack(slab, factors)
     coded_input = code_stack(block_input, lifts_all)
     return lax.psum_scatter(

time: 1260 us -> 1320 us (1.048)
  waiting for transfers between devices: 918 us -> 969 us
    all_gather x1 -> x0, waiting for transfers between devices: 154 us -> none  [per_device(): block_input = lax.all_gather(activation, 'mem', axis=1, tiled=True)]
    all_to_all x0 -> x1, waiting for transfers between devices: none -> 124 us  [per_device(): all_to_all(jnp.stack([activation] * psum(1, 'mem'), axis=0), 'mem', 0, 0)]
    all_to_all x1, waiting for transfers between devices: 609 us -> 692 us  [per_device(): lax.all_to_all(weight, 'mem', split_axis=1, concat_axis=2, tiled=True)]
    unnamed x3 -> x2, waiting for transfers between devices: 154 us -> 153 us
  transfers between devices with their start and end apart: 3 -> 3, of which waited for: 3 -> 3; matrix products, arithmetic and copies ran while one was open for 2% -> 7% of each run, Pallas kernels for 0% -> 0%
where the time goes in v1:
time: 1320 us
  waiting for transfers between devices  969 us (73%)
  local copies, waits for them, and re-layouts  219 us (17%)
  other arithmetic  59.6 us (5%)
  matrix products  46 us (3%)
  starting transfers between devices  13.7 us (1%)
  between operations  13.4 us (1%)
    all_to_all x1, waiting for transfers between devices, per_device(): lax.all_to_all(weight, 'mem', split_axis=1, concat_axis=2, tiled=True)  692 us
    unnamed x2, waiting for transfers between devices  153 us
    all_to_all x1, waiting for transfers between devices, per_device(): all_to_all(jnp.stack([activation] * psum(1, 'mem'), axis=0), 'mem', 0, 0)  124 us
    convert_element_type x2, local copies, waits for them, and re-layouts, code_stack(): raw_blocks[block].astype(jnp.float32)[None]  62.9 us
    convert_element_type x2, local copies, waits for them, and re-layouts, code_stack(): total = factors[:, 0, None, None] * raw_blocks[0].astype(jnp.float32)[None]  62.9 us
    unnamed x3, local copies, waits for them, and re-layouts  60.1 us
    dot_general x1, matrix products, per_device(): jnp.einsum('grk,gkc->grc', coded_weight, coded_input, preferred_element_t...  46 us
    convert_element_type x1, other arithmetic, code_stack(): total = factors[:, 0, None, None] * raw_blocks[0].astype(jnp.float32)[None]  34.1 us
  transfers between devices with their start and end apart: 3, of which 3 were waited for; matrix products, arithmetic and copies ran while one was open for 7% of the time, Pallas kernels for 0%

profile of v1, /device:TPU:0, one launch (start us, length us, event | category | flops | bytes accessed | tf_op | source)
XLA Modules:
  0.0 1320.7 jit_solution(5928210221372490084)
XLA Ops:
  6.5 5.3 stack.2
  11.8 6.4 all-to-all-start.1
  18.1 60.1 %copy.10 = bf16[2,16384,512]{2,0,1:T(2,128)(2,1)} copy(bf16[2,16384,512]{2,1,0:T(8,128)(2,1)} %param.3) | data formatting | bytes 67108864 | tf_op args[0]
  78.2 0.0 copy-start
  78.3 123.9 %all-to-all-done.1 = bf16[8,2,512,512]{3,2,1,0:T(8,128)(2,1)} async-done(((bf16[8,2,512,512]{3,2,1,0:T(8,128)(2,1)}), bf16[8,2,512,512]{3,2,1,0:T(8,128)(2,1)}, u32[]{:S(2)}, u32[]{:S(2)}) %all-to-all-start.1) | async-done | bytes 8388640 | tf_op jit(solution)/shard_map/all_to_all | solution.py:24
  202.1 7.1 all-to-all-start
  209.2 0.2 reduce-scatter.4.cloned.1.call-start
  209.4 0.0 copy-done
  209.5 0.1 broadcast_power_fusion
  209.6 5.3 fusion.9
  214.8 10.4 bitcast_convert_fusion
  225.3 15.1 %add_convert_fusion.10 = bf16[4,4096,512]{2,1,0:T(8,128)(2,1)} fusion(f32[4096,512]{1,0:T(8,128)} %get-tuple-element.17, f32[4]{0:T(128)S(1)} %get-tuple-element.10, f32[4096,512]{1,0:T(8,128)} %get-tuple-element.18, f32[4]{0:T(128)S(1)} %get-tuple-element.9), kind=kLoop, calls=%fused_computation.6.clone.clone.2 | loop fusion | flops 33554432 | bytes 33554464 | tf_op jit(solution)/shard_map/grk,gkc->grc/dot_general | solution.py:29
  240.4 692.0 %all-to-all-done = bf16[2,16384,512]{2,0,1:T(2,128)(2,1)} async-done(((bf16[2,16384,512]{2,0,1:T(2,128)(2,1)}), bf16[2,16384,512]{2,0,1:T(2,128)(2,1)}, u32[]{:S(2)}, u32[]{:S(2)}) %all-to-all-start) | async-done | bytes 33554464 | tf_op jit(solution)/shard_map/all_to_all | solution.py:22
  932.4 22.7 %copy.11 = bf16[2,16384,512]{2,1,0:T(8,128)(2,1)} copy(bf16[2,16384,512]{2,0,1:T(2,128)(2,1)} %all-to-all-done) | data formatting | bytes 67108864 | tf_op jit(solution)/shard_map/all_to_all | solution.py:22
  955.1 34.1 %slice_convert_fusion.1 = (f32[1,2048,8,512]{3,1,2,0:T(8,128)}, f32[1,2048,8,512]{3,1,2,0:T(8,128)}) fusion(bf16[2,2048,8,512]{3,1,2,0:T(8,128)(2,1)} %bitcast.22), kind=kLoop, calls=%fused_computation.8 | loop fusion | flops 16777216 | bytes 100663296 | tf_op jit(solution)/shard_map/convert_element_type | solution.py:9
  989.1 31.8 %copy.14 = f32[1,2048,8,512]{1,3,2,0:T(8,128)} copy(f32[1,2048,8,512]{3,1,2,0:T(8,128)} %get-tuple-element.6) | data formatting | bytes 67108864 | tf_op jit(solution)/shard_map/convert_element_type | solution.py:11
  1020.9 31.1 %copy.15 = f32[2048,4096]{1,0:T(8,128)} copy(f32[2048,4096]{0,1:T(8,128)} %bitcast.23) | data formatting | bytes 67108864 | tf_op jit(solution)/shard_map/convert_element_type | solution.py:11
  1052.0 31.8 %copy.12 = f32[1,2048,8,512]{1,3,2,0:T(8,128)} copy(f32[1,2048,8,512]{3,1,2,0:T(8,128)} %get-tuple-element.5) | data formatting | bytes 67108864 | tf_op jit(solution)/shard_map/convert_element_type | solution.py:9
  1083.8 31.1 %copy.13 = f32[2048,4096]{1,0:T(8,128)} copy(f32[2048,4096]{0,1:T(8,128)} %bitcast.24) | data formatting | bytes 67108864 | tf_op jit(solution)/shard_map/convert_element_type | solution.py:9
  1114.9 46.0 %fusion = f32[4,2048,512]{2,1,0:T(8,128)} fusion(f32[2048,4096]{1,0:T(8,128)} %copy.15, f32[4]{0:T(128)S(1)} %get-tuple-element.15, f32[2048,4096]{1,0:T(8,128)} %copy.13, f32[4]{0:T(128)S(1)} %get-tuple-element.16, bf16[4,4096,512]{2,1,0:T(8,128)(2,1)} %add_convert_fusion.10), kind=kOutput, calls=%fused_computation.1 | convolution fusion | flops 34493956096 | bytes 100663328 | tf_op jit(solution)/shard_map/grk,gkc->grc/dot_general | solution.py:29
  1161.0 0.0 reduce-scatter.4.cloned.1.call-update
  1161.0 152.8 %reduce-scatter.4.cloned.1.call-done = f32[1,2048,512]{2,1,0:T(8,128)} async-done(((f32[4,2048,512]{2,1,0:T(8,128)}), f32[1,2048,512]{2,1,0:T(8,128)}) %reduce-scatter.4.cloned.1.call-update) | async-done | bytes 4194320
  (3 shorter events, 0.0 us)
Async XLA Ops:
  11.8 190.3 %all-to-all-start.1 = ((bf16[8,2,512,512]{3,2,1,0:T(8,128)(2,1)}), bf16[8,2,512,512]{3,2,1,0:T(8,128)(2,1)}, u32[]{:S(2)}, u32[]{:S(2)}) async-start(bf16[8,2,512,512]{3,2,1,0:T(8,128)(2,1)} %stack.2), calls=%async_computation.1 | async-start | bytes 16777216 | tf_op jit(solution)/shard_map/all_to_all | solution.py:24
  78.2 131.2 %copy-start = (s32[4]{0:T(128)S(1)}, s32[4]{0:T(128)}, u32[]{:S(2)}) copy-start(s32[4]{0:T(128)} %param.5) | copy-start | bytes 52
  202.1 730.3 %all-to-all-start = ((bf16[2,16384,512]{2,0,1:T(2,128)(2,1)}), bf16[2,16384,512]{2,0,1:T(2,128)(2,1)}, u32[]{:S(2)}, u32[]{:S(2)}) async-start(bf16[2,16384,512]{2,0,1:T(2,128)(2,1)} %copy.10), calls=%async_computation | async-start | bytes 67108864 | tf_op jit(solution)/shard_map/all_to_all | solution.py:22
  209.2 1104.6 %reduce-scatter.4.cloned.1.call-start = ((), (), s32[]{:S(2)}) async-start(), calls=%async_computation.3 | async-start | bytes 20971520
Sparse Core Ops, SparseCore 0:
  1161.1 152.6 reduce-scatter.3

commit v2 on v0

--- a/solution.py
+++ b/solution.py
@@ -18,7 +18,10 @@
     anchors = (points + 1).astype(jnp.float32) / groups
     factors = anchors[:, None] ** jnp.arange(blocks, dtype=jnp.float32)[None, :]
     lifts_all = anchors[:, None] ** (jnp.arange(splits, dtype=jnp.float32) * blocks)[None, :]
-    slab = lax.all_to_all(weight, "mem", split_axis=1, concat_axis=2, tiled=True)
+    size = lax.axis_size("mem")
+    pieces = jnp.stack(jnp.split(weight, size, axis=1), axis=0)
+    pieces = lax.all_to_all(pieces, "mem", split_axis=0, concat_axis=0)
+    slab = jnp.concatenate(pieces, axis=2)
     block_input = lax.all_gather(activation, "mem", axis=1, tiled=True)
     coded_weight = code_stack(slab, factors)
     coded_input = code_stack(block_input, lifts_all)

time: 1260 us -> 1260 us (level)
    convert_element_type x2 -> x1, local copies, waits for them, and re-layouts: 62.9 us -> 31.1 us  [code_stack(): total = factors[:, 0, None, None] * raw_blocks[0].astype(jnp.float32)[None]]
    convert_element_type x2 -> x1, local copies, waits for them, and re-layouts: 62.9 us -> 31.2 us  [code_stack(): raw_blocks[block].astype(jnp.float32)[None]]
    split x0 -> x1, local copies, waits for them, and re-layouts: none -> 23.7 us  [per_device(): pieces = jnp.stack(jnp.split(weight, size, axis=1), axis=0)]
    slice x0 -> x1, local copies, waits for them, and re-layouts: none -> 23.5 us  [code_stack(): total = factors[:, 0, None, None] * raw_blocks[0].astype(jnp.float32)[None]]
    unnamed x3 -> x27, local copies, waits for them, and re-layouts: 60.1 us -> 75.1 us
where the time goes in v2:
time: 1260 us
  waiting for transfers between devices  918 us (73%)
  local copies, waits for them, and re-layouts  210 us (17%)
  other arithmetic  60.7 us (5%)
  matrix products  46 us (4%)
  between operations  13.5 us (1%)
    all_to_all x1, waiting for transfers between devices, per_device(): pieces = lax.all_to_all(pieces, 'mem', split_axis=0, concat_axis=0)  609 us
    all_gather x1, waiting for transfers between devices, per_device(): block_input = lax.all_gather(activation, 'mem', axis=1, tiled=True)  154 us
    unnamed x3, waiting for transfers between devices  154 us
    unnamed x27, local copies, waits for them, and re-layouts  75.1 us
    dot_general x1, matrix products, per_device(): jnp.einsum('grk,gkc->grc', coded_weight, coded_input, preferred_element_t...  46 us
    convert_element_type x1, other arithmetic, code_stack(): raw_blocks[block].astype(jnp.float32)[None]  33.8 us
    convert_element_type x1, local copies, waits for them, and re-layouts, code_stack(): raw_blocks[block].astype(jnp.float32)[None]  31.2 us
    convert_element_type x1, local copies, waits for them, and re-layouts, code_stack(): total = factors[:, 0, None, None] * raw_blocks[0].astype(jnp.float32)[None]  31.1 us
  transfers between devices with their start and end apart: 3, of which 3 were waited for; matrix products, arithmetic and copies ran while one was open for 2% of the time, Pallas kernels for 0%

profile of v2, /device:TPU:0, one launch (start us, length us, event | category | flops | bytes accessed | tf_op | source)
XLA Modules:
  0.0 1255.1 jit_solution(18180500791674269142)
XLA Ops:
  6.5 23.7 %fusion.12 = (bf16[2,2048,512]{2,1,0:T(8,128)(2,1)}, bf16[2,2048,512]{2,1,0:T(8,128)(2,1)}, bf16[2,2048,512]{2,1,0:T(8,128)(2,1)}, bf16[2,2048,512]{2,1,0:T(8,12...) fusion(bf16[2,16384,512]{2,1,0:T(8,128)(2,1)} %param.3), kind=kLoop, calls=%fused_computation.35 | loop fusion | bytes 67108864 | tf_op jit(solution)/shard_map/split | solution.py:22
  30.3 6.3 copy.25
  36.6 4.7 bitcast_dynamic-update-slice_fusion.7
  41.4 6.3 copy.26
  47.6 6.3 copy.27
  54.0 6.3 copy.28
  60.3 6.4 copy.29
  66.6 6.3 copy.30
  72.9 6.3 copy.31
  79.2 6.3 copy.32
  85.5 0.0 copy-start.4
  85.5 0.0 copy-start.3
  85.5 0.0 copy-start.2
  85.5 5.1 bitcast_dynamic-update-slice_fusion.6
  90.5 0.0 copy-start
  90.5 5.5 bitcast_dynamic-update-slice_fusion.5
  96.1 0.0 copy-done.4
  96.1 0.0 copy-start.1
  96.1 2.4 bitcast_dynamic-update-slice_fusion.4
  98.5 0.0 copy-done.3
  98.5 2.3 bitcast_dynamic-update-slice_fusion.3
  100.8 0.0 copy-done.2
  100.8 2.3 bitcast_dynamic-update-slice_fusion.2
  103.1 0.0 copy-done
  103.1 2.3 bitcast_dynamic-update-slice_fusion.1
  105.4 0.0 copy-done.1
  105.4 2.2 bitcast_dynamic-update-slice_fusion
  107.6 0.0 copy-start.5
  107.6 7.3 all-to-all-start
  115.0 0.0 all-gather.2.cloned.1.call-start
  115.0 0.7 all-gather.2.cloned.1.call-update
  115.7 0.2 reduce-scatter.4.cloned.1.call-start
  115.9 0.0 copy-done.5
  116.0 0.1 broadcast_power_fusion
  116.1 154.3 %all-gather.2.cloned.1.call-done = bf16[2,4096,512]{2,1,0:T(8,128)(2,1)} async-done(((bf16[2,512,512]{2,1,0:T(8,128)(2,1)}), bf16[2,4096,512]{2,1,0:T(8,128)(2,1)}) %all-gather.2.cloned.1.call-update) | async-done | bytes 8388624 | tf_op jit(solution)/shard_map/all_gather | solution.py:25
  270.3 11.7 fusion.10
  282.0 15.1 %add_convert_fusion.10 = bf16[4,4096,512]{2,1,0:T(8,128)(2,1)} fusion(f32[4096,512]{1,0:T(8,128)} %get-tuple-element.16, f32[4]{0:T(128)S(1)} %get-tuple-element.18, f32[4096,512]{1,0:T(8,128)} %get-tuple-element.15, f32[4]{0:T(128)S(1)} %get-tuple-element.17), kind=kLoop, calls=%fused_computation.7.clone.clone.2 | loop fusion | flops 33554432 | bytes 33554464 | tf_op jit(solution)/shard_map/grk,gkc->grc/dot_general | solution.py:29
  297.2 609.1 %all-to-all-done = bf16[8,2,2048,512]{2,3,1,0:T(8,128)(2,1)} async-done(((bf16[8,2,2048,512]{2,3,1,0:T(8,128)(2,1)}), bf16[8,2,2048,512]{2,3,1,0:T(8,128)(2,1)}, u32[]{:S(2)}, u32[]{:S(2)}) %all-to-all-start) | async-done | bytes 33554464 | tf_op jit(solution)/shard_map/all_to_all | solution.py:23
  906.3 22.8 %copy.34 = bf16[8,2,2048,512]{2,3,0,1:T(8,128)(2,1)} copy(bf16[8,2,2048,512]{2,3,1,0:T(8,128)(2,1)} %all-to-all-done) | data formatting | bytes 67108864 | tf_op jit(solution)/shard_map/all_to_all | solution.py:23
  929.1 23.5 %fusion.11 = (bf16[1,2048,8,512]{1,3,2,0:T(8,128)(2,1)}, bf16[1,2048,8,512]{1,3,2,0:T(8,128)(2,1)}) fusion(bf16[2,2048,8,512]{1,3,2,0:T(8,128)(2,1)} %bitcast.45), kind=kLoop, calls=%fused_computation.34 | loop fusion | bytes 67108864 | tf_op jit(solution)/shard_map/slice | solution.py:8
  952.6 33.8 %bitcast_convert_fusion = (f32[2048,4096]{0,1:T(8,128)}, f32[2048,4096]{0,1:T(8,128)}) fusion(bf16[1,2048,8,512]{1,3,2,0:T(8,128)(2,1)} %get-tuple-element.6, bf16[1,2048,8,512]{1,3,2,0:T(8,128)(2,1)} %get-tuple-element.5), kind=kLoop, calls=%fused_computation.8 | loop fusion | flops 16777216 | bytes 100663296 | tf_op jit(solution)/shard_map/convert_element_type | solution.py:10
  986.4 31.1 %copy.23 = f32[2048,4096]{1,0:T(8,128)} copy(f32[2048,4096]{0,1:T(8,128)} %get-tuple-element.24) | data formatting | bytes 67108864 | tf_op jit(solution)/shard_map/convert_element_type | solution.py:8
  1017.5 31.2 %copy.24 = f32[2048,4096]{1,0:T(8,128)} copy(f32[2048,4096]{0,1:T(8,128)} %get-tuple-element.23) | data formatting | bytes 67108864 | tf_op jit(solution)/shard_map/convert_element_type | solution.py:10
  1048.7 46.0 %fusion = f32[4,2048,512]{2,1,0:T(8,128)} fusion(f32[2048,4096]{1,0:T(8,128)} %copy.24, f32[4]{0:T(128)S(1)} %get-tuple-element.25, f32[2048,4096]{1,0:T(8,128)} %copy.23, f32[4]{0:T(128)S(1)} %get-tuple-element.26, bf16[4,4096,512]{2,1,0:T(8,128)(2,1)} %add_convert_fusion.10), kind=kOutput, calls=%fused_computation.1 | convolution fusion | flops 34493956096 | bytes 100663328 | tf_op jit(solution)/shard_map/grk,gkc->grc/dot_general | solution.py:29
  1094.7 0.0 reduce-scatter.4.cloned.1.call-update
  1094.8 153.5 %reduce-scatter.4.cloned.1.call-done = f32[1,2048,512]{2,1,0:T(8,128)} async-done(((f32[4,2048,512]{2,1,0:T(8,128)}), f32[1,2048,512]{2,1,0:T(8,128)}) %reduce-scatter.4.cloned.1.call-update) | async-done | bytes 4194320
  (3 shorter events, 0.0 us)
Async XLA Ops:
  85.5 10.6 copy-start.4
  85.5 13.1 %copy-start.3 = (bf16[2,2048,512]{1,2,0:T(8,128)(2,1)S(1)}, bf16[2,2048,512]{1,2,0:T(8,128)(2,1)}, u32[]{:S(2)}) copy-start(bf16[2,2048,512]{1,2,0:T(8,128)(2,1)} %copy.29) | copy-start | bytes 12582916
  85.5 15.3 %copy-start.2 = (bf16[2,2048,512]{1,2,0:T(8,128)(2,1)S(1)}, bf16[2,2048,512]{1,2,0:T(8,128)(2,1)}, u32[]{:S(2)}) copy-start(bf16[2,2048,512]{1,2,0:T(8,128)(2,1)} %copy.30) | copy-start | bytes 12582916
  90.5 12.6 %copy-start = (bf16[2,2048,512]{1,2,0:T(8,128)(2,1)S(1)}, bf16[2,2048,512]{1,2,0:T(8,128)(2,1)}, u32[]{:S(2)}) copy-start(bf16[2,2048,512]{1,2,0:T(8,128)(2,1)} %copy.31) | copy-start | bytes 12582916
  96.1 9.3 copy-start.1
  107.6 8.3 copy-start.5
  107.6 798.7 %all-to-all-start = ((bf16[8,2,2048,512]{2,3,1,0:T(8,128)(2,1)}), bf16[8,2,2048,512]{2,3,1,0:T(8,128)(2,1)}, u32[]{:S(2)}, u32[]{:S(2)}) async-start(bf16[8,2,2048,512]{2,3,1,0:T(8,128)(2,1)} %bitcast_dynamic-update-slice_fusion), calls=%async_computation | async-start | bytes 67108864 | tf_op jit(solution)/shard_map/all_to_all | solution.py:23
  115.0 155.4 %all-gather.2.cloned.1.call-start = ((), (), s32[]{:S(2)}) async-start(), calls=%async_computation.2 | async-start | bytes 9437184 | tf_op jit(solution)/shard_map/all_gather | solution.py:25
  115.7 1132.6 %reduce-scatter.4.cloned.1.call-start = ((), (), s32[]{:S(2)}) async-start(), calls=%async_computation.3 | async-start | bytes 20971520
Sparse Core Ops, SparseCore 0:
  117.4 152.9 all-gather.1
  1094.9 153.3 reduce-scatter.3
